TPU v7x, 32 devices: a whole 2x2x4 slice. The times are simulated.
32 devices in a mesh: section: 4 (over y, x), stem: 8 (over z, core).
Axes of the slice: x: 2, y: 2, z: 4, core: 2. Of those that a mesh axis runs over, the one named last changes fastest.
Arguments:
- bitstrings: int32 [4, 4, 32, 3], P('section'), may hold values 0 or 1
- boundary: float32 [2, 2048], replicated, may hold values from -6 to 6
- stem_tensor: float32 [4, 2, 2048, 8, 2048], P('section', None, 'stem'), may hold values from -0.09375 to 0.09375
- probe_vectors: float32 [4, 2, 2048], P('section'), may hold values from -0.09375 to 0.09375
- inbound_permutations: int32 [4, 2048], replicated, may hold values from 0 to 2047, each once within a row
Outputs:
- amplitudes: float32 [4, 2, 4, 32], P('section')
Inputs may be any that keep to these rules, and one draw needn't show every extreme that they name: `inbound_permutations`: each row of relabeling names every number of 0 to 2047 once.
All inputs are finite; a program needn't handle non-finite values. No bound on the sum of `bitstrings` on one device may be relied on, other than what follows from the above.
Results may differ from a plain program's by a relative error of at most 0.0003.
Values sent between devices are 32-bit elements; how exact they have to be, the bound alone decides.
No kernel may reach another device: no remote copies, remote signals or barrier semaphores. Data moves between devices by JAX's collectives and lax.ppermute only.
A program may use at most 128 MiB of HBM per device.

v0:
```python
import jax
import jax.numpy as jnp
from jax import lax
from jax.sharding import PartitionSpec as P


def from_behind(block, axis, distance):
    devices = range(lax.axis_size(axis))
    route = [(i - distance, i) for i in devices if i - distance in devices]
    return lax.ppermute(block, axis, route)


def local(bitstrings, boundary, stem_tensor, probe_vectors, inbound_permutations):
    section_count = lax.axis_size("section")
    segment_ordinal = lax.axis_index("section")
    stem_rank = lax.axis_index("stem")
    local_rows = stem_tensor.shape[2]
    settings_count = stem_tensor.shape[3]
    width = stem_tensor.shape[4]
    micro_count = bitstrings.shape[1]
    batch_size = bitstrings.shape[2]
    qubit_count = bitstrings.shape[3]
    powers = jnp.left_shift(jnp.int32(1), jnp.arange(qubit_count, dtype=jnp.int32))
    bit_patterns = jnp.sum(bitstrings[0] * powers, axis=-1)
    weight_real = stem_tensor[0, 0].reshape(local_rows * settings_count, width)
    weight_imag = stem_tensor[0, 1].reshape(local_rows * settings_count, width)
    own_perm = lax.dynamic_index_in_dim(inbound_permutations, segment_ordinal, 0, False)
    row_ids = lax.dynamic_slice_in_dim(own_perm, stem_rank * local_rows, local_rows)
    start_state = jnp.broadcast_to(
        jnp.take(boundary, row_ids, axis=1)[:, None, :], (2, batch_size, local_rows)
    )
    probe_re = probe_vectors[0, 0]
    probe_im = probe_vectors[0, 1]
    setting_ids = jnp.arange(settings_count, dtype=jnp.int32)

    def advance(moment, state_pair):
        incoming, buffer = state_pair
        position = moment - segment_ordinal
        active = jnp.logical_and(position >= 0, position < micro_count)
        clipped = jnp.clip(position, 0, micro_count - 1)
        pattern = lax.dynamic_index_in_dim(bit_patterns, clipped, 0, False)
        gathered = lax.all_gather(incoming, "stem", axis=2, tiled=True)
        arriving = jnp.take(gathered, row_ids, axis=2)
        current = jnp.where(segment_ordinal == 0, start_state, arriving)
        onehot = (setting_ids[None, :] == pattern[:, None]).astype(jnp.float32)
        expanded = (current[:, :, :, None] * onehot[None, :, None, :]).reshape(
            2 * batch_size, local_rows * settings_count
        )
        prod_real = jnp.dot(expanded, weight_real, precision=lax.Precision.HIGHEST)
        prod_imag = jnp.dot(expanded, weight_imag, precision=lax.Precision.HIGHEST)
        out_real = prod_real[:batch_size] - prod_imag[batch_size:]
        out_imag = prod_imag[:batch_size] + prod_real[batch_size:]
        partial_value = jnp.stack([out_real, out_imag])
        term_real = jnp.dot(out_real, probe_re, precision=lax.Precision.HIGHEST) - jnp.dot(
            out_imag, probe_im, precision=lax.Precision.HIGHEST
        )
        term_imag = jnp.dot(out_real, probe_im, precision=lax.Precision.HIGHEST) + jnp.dot(
            out_imag, probe_re, precision=lax.Precision.HIGHEST
        )
        intersection_terms = jnp.stack([term_real, term_imag])[:, None, :]
        previous = lax.dynamic_slice_in_dim(buffer, clipped, 1, 1)
        updated = jnp.where(active, intersection_terms, previous)
        buffer = lax.dynamic_update_slice_in_dim(buffer, updated, clipped, 1)
        summed = lax.psum_scatter(partial_value, "stem", scatter_dimension=2, tiled=True)
        incoming = from_behind(summed, "section", 1)
        return (incoming, buffer)

    initial_incoming = jnp.zeros((2, batch_size, local_rows), jnp.float32)
    first_buffer = jnp.zeros((2, micro_count, batch_size), jnp.float32)
    time_steps = micro_count + section_count - 1
    final_incoming, buffer = lax.fori_loop(0, time_steps, advance, (initial_incoming, first_buffer))
    amplitudes = lax.psum(buffer, "stem")
    return amplitudes[None]


def solution(mesh):
    return jax.shard_map(
        local,
        mesh=mesh,
        in_specs=(
            P("section", None, None, None),
            P(),
            P("section", None, "stem", None, None),
            P("section", None, None),
            P(),
        ),
        out_specs=P("section", None, None, None),
        check_vma=False,
    )
```

profile of v0, /device:TPU:5, one launch (start us, length us, event | category | flops | bytes accessed | tf_op | source)
XLA Modules:
  0.0 622.9 jit_solution(6774410743164879172)
XLA Ops:
  9.3 21.2 %slice_bitcast_fusion = (f32[2048,2048]{1,0:T(8,128)}, f32[2048,2048]{1,0:T(8,128)}) fusion(f32[1,2,256,8,2048]{4,3,2,1,0:T(8,128)} %param.9), kind=kLoop, calls=%fused_computation.29 | loop fusion | bytes 67108864 | tf_op jit(solution)/shard_map/reshape;squeeze | solution.py:26
  30.6 567.1 %while.17 = (s32[]{:T(128)}, f32[2,32,256]{2,1,0:T(8,128)S(1)}, f32[2,4,32]{2,1,0:T(4,128)S(1)}, pred[]{:T(512)}, s32[256]{0:T(256)S(1)}, /*index=5*/s32[]{:T(12...) while((s32[]{:T(128)}, f32[2,32,256]{2,1,0:T(8,128)S(1)}, ...), condition=%wide.region_3.4_spmd.clone, body=%wide.region_1.3_spmd.clone.sunk | while | flops 6446288896 | bytes 113100216 | solution.py:71
  30.7 15.6 %all_gather.10 = f32[2,32,2048]{2,1,0:T(8,128)S(1)} all-gather(f32[2,32,256]{2,1,0:T(8,128)S(1)} %get-tuple-element.424), channel_id=1, replica_groups=mesh['section'=4,'stem'=8] {'stem'}, dimensions={2}, use_global_device_ids=true | all-gather | bytes 589824 | tf_op jit(solution)/shard_map/while/body/eval_jaxpr/all_gather | solution.py:42
  51.3 13.9 %fusion.48 = f32[64,2048]{1,0:T(8,128)S(1)} fusion(f32[64,2048]{0,1:T(8,128)S(1)} %mul.72, f32[2048,2048]{1,0:T(8,128)} %get-tuple-element.447), kind=kOutput, calls=%fused_computation.41.clone.1 | convolution fusion | flops 3221225472 | bytes 17825792 | tf_op jit(solution)/shard_map/while/body/eval_jaxpr/dot_general | solution.py:50
  77.7 27.5 %reduce-scatter.2.cloned.1.call-done = f32[2,32,256]{2,1,0:T(8,128)} async-done(((f32[2,32,2048]{2,1,0:T(8,128)}), f32[2,32,256]{2,1,0:T(8,128)}) %reduce-scatter.2.cloned.1.call-update) | async-done | bytes 65552 | tf_op jit(solution)/shard_map/while/body/eval_jaxpr/reduce_scatter | solution.py:64
  111.3 19.5 %all_gather.10 = f32[2,32,2048]{2,1,0:T(8,128)S(1)} all-gather(f32[2,32,256]{2,1,0:T(8,128)S(1)} %get-tuple-element.424), channel_id=1, replica_groups=mesh['section'=4,'stem'=8] {'stem'}, dimensions={2}, use_global_device_ids=true | all-gather | bytes 589824 | tf_op jit(solution)/shard_map/while/body/eval_jaxpr/all_gather | solution.py:42
  135.8 13.9 %fusion.48 = f32[64,2048]{1,0:T(8,128)S(1)} fusion(f32[64,2048]{0,1:T(8,128)S(1)} %mul.72, f32[2048,2048]{1,0:T(8,128)} %get-tuple-element.447), kind=kOutput, calls=%fused_computation.41.clone.1 | convolution fusion | flops 3221225472 | bytes 17825792 | tf_op jit(solution)/shard_map/while/body/eval_jaxpr/dot_general | solution.py:50
  162.2 24.0 %reduce-scatter.2.cloned.1.call-done = f32[2,32,256]{2,1,0:T(8,128)} async-done(((f32[2,32,2048]{2,1,0:T(8,128)}), f32[2,32,256]{2,1,0:T(8,128)}) %reduce-scatter.2.cloned.1.call-update) | async-done | bytes 65552 | tf_op jit(solution)/shard_map/while/body/eval_jaxpr/reduce_scatter | solution.py:64
  192.3 19.5 %all_gather.10 = f32[2,32,2048]{2,1,0:T(8,128)S(1)} all-gather(f32[2,32,256]{2,1,0:T(8,128)S(1)} %get-tuple-element.424), channel_id=1, replica_groups=mesh['section'=4,'stem'=8] {'stem'}, dimensions={2}, use_global_device_ids=true | all-gather | bytes 589824 | tf_op jit(solution)/shard_map/while/body/eval_jaxpr/all_gather | solution.py:42
  216.8 13.9 %fusion.48 = f32[64,2048]{1,0:T(8,128)S(1)} fusion(f32[64,2048]{0,1:T(8,128)S(1)} %mul.72, f32[2048,2048]{1,0:T(8,128)} %get-tuple-element.447), kind=kOutput, calls=%fused_computation.41.clone.1 | convolution fusion | flops 3221225472 | bytes 17825792 | tf_op jit(solution)/shard_map/while/body/eval_jaxpr/dot_general | solution.py:50
  243.2 24.1 %reduce-scatter.2.cloned.1.call-done = f32[2,32,256]{2,1,0:T(8,128)} async-done(((f32[2,32,2048]{2,1,0:T(8,128)}), f32[2,32,256]{2,1,0:T(8,128)}) %reduce-scatter.2.cloned.1.call-update) | async-done | bytes 65552 | tf_op jit(solution)/shard_map/while/body/eval_jaxpr/reduce_scatter | solution.py:64
  273.5 19.5 %all_gather.10 = f32[2,32,2048]{2,1,0:T(8,128)S(1)} all-gather(f32[2,32,256]{2,1,0:T(8,128)S(1)} %get-tuple-element.424), channel_id=1, replica_groups=mesh['section'=4,'stem'=8] {'stem'}, dimensions={2}, use_global_device_ids=true | all-gather | bytes 589824 | tf_op jit(solution)/shard_map/while/body/eval_jaxpr/all_gather | solution.py:42
  298.0 13.9 %fusion.48 = f32[64,2048]{1,0:T(8,128)S(1)} fusion(f32[64,2048]{0,1:T(8,128)S(1)} %mul.72, f32[2048,2048]{1,0:T(8,128)} %get-tuple-element.447), kind=kOutput, calls=%fused_computation.41.clone.1 | convolution fusion | flops 3221225472 | bytes 17825792 | tf_op jit(solution)/shard_map/while/body/eval_jaxpr/dot_general | solution.py:50
  324.4 24.0 %reduce-scatter.2.cloned.1.call-done = f32[2,32,256]{2,1,0:T(8,128)} async-done(((f32[2,32,2048]{2,1,0:T(8,128)}), f32[2,32,256]{2,1,0:T(8,128)}) %reduce-scatter.2.cloned.1.call-update) | async-done | bytes 65552 | tf_op jit(solution)/shard_map/while/body/eval_jaxpr/reduce_scatter | solution.py:64
  354.5 19.5 %all_gather.10 = f32[2,32,2048]{2,1,0:T(8,128)S(1)} all-gather(f32[2,32,256]{2,1,0:T(8,128)S(1)} %get-tuple-element.424), channel_id=1, replica_groups=mesh['section'=4,'stem'=8] {'stem'}, dimensions={2}, use_global_device_ids=true | all-gather | bytes 589824 | tf_op jit(solution)/shard_map/while/body/eval_jaxpr/all_gather | solution.py:42
  379.0 13.9 %fusion.48 = f32[64,2048]{1,0:T(8,128)S(1)} fusion(f32[64,2048]{0,1:T(8,128)S(1)} %mul.72, f32[2048,2048]{1,0:T(8,128)} %get-tuple-element.447), kind=kOutput, calls=%fused_computation.41.clone.1 | convolution fusion | flops 3221225472 | bytes 17825792 | tf_op jit(solution)/shard_map/while/body/eval_jaxpr/dot_general | solution.py:50
  405.4 24.1 %reduce-scatter.2.cloned.1.call-done = f32[2,32,256]{2,1,0:T(8,128)} async-done(((f32[2,32,2048]{2,1,0:T(8,128)}), f32[2,32,256]{2,1,0:T(8,128)}) %reduce-scatter.2.cloned.1.call-update) | async-done | bytes 65552 | tf_op jit(solution)/shard_map/while/body/eval_jaxpr/reduce_scatter | solution.py:64
  435.7 19.5 %all_gather.10 = f32[2,32,2048]{2,1,0:T(8,128)S(1)} all-gather(f32[2,32,256]{2,1,0:T(8,128)S(1)} %get-tuple-element.424), channel_id=1, replica_groups=mesh['section'=4,'stem'=8] {'stem'}, dimensions={2}, use_global_device_ids=true | all-gather | bytes 589824 | tf_op jit(solution)/shard_map/while/body/eval_jaxpr/all_gather | solution.py:42
  460.2 13.9 %fusion.48 = f32[64,2048]{1,0:T(8,128)S(1)} fusion(f32[64,2048]{0,1:T(8,128)S(1)} %mul.72, f32[2048,2048]{1,0:T(8,128)} %get-tuple-element.447), kind=kOutput, calls=%fused_computation.41.clone.1 | convolution fusion | flops 3221225472 | bytes 17825792 | tf_op jit(solution)/shard_map/while/body/eval_jaxpr/dot_general | solution.py:50
  486.6 24.0 %reduce-scatter.2.cloned.1.call-done = f32[2,32,256]{2,1,0:T(8,128)} async-done(((f32[2,32,2048]{2,1,0:T(8,128)}), f32[2,32,256]{2,1,0:T(8,128)}) %reduce-scatter.2.cloned.1.call-update) | async-done | bytes 65552 | tf_op jit(solution)/shard_map/while/body/eval_jaxpr/reduce_scatter | solution.py:64
  516.7 19.5 %all_gather.10 = f32[2,32,2048]{2,1,0:T(8,128)S(1)} all-gather(f32[2,32,256]{2,1,0:T(8,128)S(1)} %get-tuple-element.424), channel_id=1, replica_groups=mesh['section'=4,'stem'=8] {'stem'}, dimensions={2}, use_global_device_ids=true | all-gather | bytes 589824 | tf_op jit(solution)/shard_map/while/body/eval_jaxpr/all_gather | solution.py:42
  541.2 13.9 %fusion.48 = f32[64,2048]{1,0:T(8,128)S(1)} fusion(f32[64,2048]{0,1:T(8,128)S(1)} %mul.72, f32[2048,2048]{1,0:T(8,128)} %get-tuple-element.447), kind=kOutput, calls=%fused_computation.41.clone.1 | convolution fusion | flops 3221225472 | bytes 17825792 | tf_op jit(solution)/shard_map/while/body/eval_jaxpr/dot_general | solution.py:50
  567.6 24.0 %reduce-scatter.2.cloned.1.call-done = f32[2,32,256]{2,1,0:T(8,128)} async-done(((f32[2,32,2048]{2,1,0:T(8,128)}), f32[2,32,256]{2,1,0:T(8,128)}) %reduce-scatter.2.cloned.1.call-update) | async-done | bytes 65552 | tf_op jit(solution)/shard_map/while/body/eval_jaxpr/reduce_scatter | solution.py:64
  597.7 18.4 %psum.7 = f32[1,2,4,32]{3,2,1,0:T(4,128)} all-reduce(f32[1,2,4,32]{3,2,1,0:T(4,128)S(1)} %bitcast.124), channel_id=1, replica_groups=mesh['section'=4,'stem'=8] {'stem'}, use_global_device_ids=true, to_apply=%region_4.5 | all-reduce | flops 256 | bytes 2048 | tf_op jit(solution)/shard_map/psum | solution.py:72
  (197 shorter events, 167.3 us)
Async XLA Ops:
  9.3 21.2 %copy-start.1 = (f32[1,2,2048]{2,1,0:T(2,128)S(1)}, f32[1,2,2048]{2,1,0:T(2,128)}, u32[]{:S(2)}) copy-start(f32[1,2,2048]{2,1,0:T(2,128)} %param.10) | copy-start | bytes 49156
  9.3 21.2 %copy-start.2 = (s32[1,4,32,3]{2,1,3,0:T(4,128)S(1)}, s32[1,4,32,3]{2,1,3,0:T(4,128)}, u32[]{:S(2)}) copy-start(s32[1,4,32,3]{2,1,3,0:T(4,128)} %param.7) | copy-start | bytes 4612
  30.6 74.5 %reduce-scatter.2.cloned.1.call-start = ((), (), s32[]{:S(2)}) async-start(), calls=%async_computation.1 | async-start | bytes 589824 | tf_op jit(solution)/shard_map/while/body/eval_jaxpr/reduce_scatter | solution.py:64
  51.2 13.9 %copy-start = (f32[2048,2048]{1,0:T(8,128)S(1)}, f32[2048,2048]{1,0:T(8,128)}, u32[]{:S(2)}) copy-start(f32[2048,2048]{1,0:T(8,128)} %get-tuple-element.446) | copy-start | bytes 50331652 | tf_op jit(solution)/shard_map/while
  105.1 6.1 collective-permute-start
  111.2 74.9 %reduce-scatter.2.cloned.1.call-start = ((), (), s32[]{:S(2)}) async-start(), calls=%async_computation.1 | async-start | bytes 589824 | tf_op jit(solution)/shard_map/while/body/eval_jaxpr/reduce_scatter | solution.py:64
  135.8 13.9 %copy-start = (f32[2048,2048]{1,0:T(8,128)S(1)}, f32[2048,2048]{1,0:T(8,128)}, u32[]{:S(2)}) copy-start(f32[2048,2048]{1,0:T(8,128)} %get-tuple-element.446) | copy-start | bytes 50331652 | tf_op jit(solution)/shard_map/while
  186.2 6.1 collective-permute-start
  192.3 75.1 %reduce-scatter.2.cloned.1.call-start = ((), (), s32[]{:S(2)}) async-start(), calls=%async_computation.1 | async-start | bytes 589824 | tf_op jit(solution)/shard_map/while/body/eval_jaxpr/reduce_scatter | solution.py:64
  216.8 13.9 %copy-start = (f32[2048,2048]{1,0:T(8,128)S(1)}, f32[2048,2048]{1,0:T(8,128)}, u32[]{:S(2)}) copy-start(f32[2048,2048]{1,0:T(8,128)} %get-tuple-element.446) | copy-start | bytes 50331652 | tf_op jit(solution)/shard_map/while
  267.3 6.1 collective-permute-start
  273.4 74.9 %reduce-scatter.2.cloned.1.call-start = ((), (), s32[]{:S(2)}) async-start(), calls=%async_computation.1 | async-start | bytes 589824 | tf_op jit(solution)/shard_map/while/body/eval_jaxpr/reduce_scatter | solution.py:64
  298.0 13.9 %copy-start = (f32[2048,2048]{1,0:T(8,128)S(1)}, f32[2048,2048]{1,0:T(8,128)}, u32[]{:S(2)}) copy-start(f32[2048,2048]{1,0:T(8,128)} %get-tuple-element.446) | copy-start | bytes 50331652 | tf_op jit(solution)/shard_map/while
  348.4 6.1 collective-permute-start
  354.5 75.1 %reduce-scatter.2.cloned.1.call-start = ((), (), s32[]{:S(2)}) async-start(), calls=%async_computation.1 | async-start | bytes 589824 | tf_op jit(solution)/shard_map/while/body/eval_jaxpr/reduce_scatter | solution.py:64
  379.0 13.9 %copy-start = (f32[2048,2048]{1,0:T(8,128)S(1)}, f32[2048,2048]{1,0:T(8,128)}, u32[]{:S(2)}) copy-start(f32[2048,2048]{1,0:T(8,128)} %get-tuple-element.446) | copy-start | bytes 50331652 | tf_op jit(solution)/shard_map/while
  429.5 6.1 collective-permute-start
  435.6 74.9 %reduce-scatter.2.cloned.1.call-start = ((), (), s32[]{:S(2)}) async-start(), calls=%async_computation.1 | async-start | bytes 589824 | tf_op jit(solution)/shard_map/while/body/eval_jaxpr/reduce_scatter | solution.py:64
  460.2 13.9 %copy-start = (f32[2048,2048]{1,0:T(8,128)S(1)}, f32[2048,2048]{1,0:T(8,128)}, u32[]{:S(2)}) copy-start(f32[2048,2048]{1,0:T(8,128)} %get-tuple-element.446) | copy-start | bytes 50331652 | tf_op jit(solution)/shard_map/while
  510.6 6.1 collective-permute-start
  516.7 74.9 %reduce-scatter.2.cloned.1.call-start = ((), (), s32[]{:S(2)}) async-start(), calls=%async_computation.1 | async-start | bytes 589824 | tf_op jit(solution)/shard_map/while/body/eval_jaxpr/reduce_scatter | solution.py:64
  541.2 13.9 %copy-start = (f32[2048,2048]{1,0:T(8,128)S(1)}, f32[2048,2048]{1,0:T(8,128)}, u32[]{:S(2)}) copy-start(f32[2048,2048]{1,0:T(8,128)} %get-tuple-element.446) | copy-start | bytes 50331652 | tf_op jit(solution)/shard_map/while
  591.6 6.1 collective-permute-start
Sparse Core Ops, SparseCore 0:
  76.4 28.6 reduce-scatter.1
  161.0 25.1 reduce-scatter.1
  242.0 25.2 reduce-scatter.1
  323.2 25.1 reduce-scatter.1
  404.2 25.2 reduce-scatter.1
  485.3 25.1 reduce-scatter.1
  566.4 25.1 reduce-scatter.1
where the time goes:
time: 623 us
  waiting for transfers between devices  192 us (31%)
  matrix products  178 us (29%)
  blocking collectives  151 us (24%)
  local copies, waits for them, and re-layouts  45.5 us (7%)
  starting transfers between devices  21.7 us (3%)
  other arithmetic  20 us (3%)
  between operations  13.5 us (2%)
    reduce_scatter x7, waiting for transfers between devices, advance(): lax.psum_scatter(partial_value, 'stem', scatter_dimension=2, tiled=True)  172 us
    all_gather x7, blocking collectives, advance(): gathered = lax.all_gather(incoming, 'stem', axis=2, tiled=True)  133 us
    dot_general x7, matrix products, advance(): prod_imag = jnp.dot(expanded, weight_imag, precision=lax.Precision.HIGHEST)  97.4 us
    dot_general x7, matrix products, advance(): prod_real = jnp.dot(expanded, weight_real, precision=lax.Precision.HIGHEST)  71.4 us
    ppermute x7, starting transfers between devices, from_behind(): return lax.ppermute(block, axis, route)  21.7 us
    another operation x1, local copies, waits for them, and re-layouts, local(): weight_imag = stem_tensor[0, 1].reshape(local_rows * settings_count, width)  21.2 us
    ppermute x7, waiting for transfers between devices, from_behind(): return lax.ppermute(block, axis, route)  20.6 us
    psum x1, blocking collectives, local(): amplitudes = lax.psum(buffer, 'stem')  18.4 us
  transfers between devices with their start and end apart: 14, of which 14 were waited for; matrix products, arithmetic and copies ran while one was open for 2% of the time, Pallas kernels for 0%

commit v1 on v0

--- a/solution.py
+++ b/solution.py
@@ -34,12 +34,31 @@
     setting_ids = jnp.arange(settings_count, dtype=jnp.int32)
 
     def advance(moment, state_pair):
+
+        def test_tails(my_tile):
+            named_axis = "stem"
+            num = lax.axis_size(named_axis)
+            gallery = [(dev_i, (dev_i + 1) % num) for dev_i in range(num)]
+
+            def end_scales_on_mesh(now):
+                if len(now) == num:
+                    return now
+                return end_scales_on_mesh(
+                    [lax.ppermute(now[0], axis_name=named_axis, perm=gallery), *now]
+                )
+
+            return jnp.roll(
+                jnp.concatenate(end_scales_on_mesh([my_tile]), 2),
+                (lax.axis_index(named_axis) + 1) * my_tile.shape[2],
+                2,
+            )
+
         incoming, buffer = state_pair
         position = moment - segment_ordinal
         active = jnp.logical_and(position >= 0, position < micro_count)
         clipped = jnp.clip(position, 0, micro_count - 1)
         pattern = lax.dynamic_index_in_dim(bit_patterns, clipped, 0, False)
-        gathered = lax.all_gather(incoming, "stem", axis=2, tiled=True)
+        gathered = test_tails(incoming)
         arriving = jnp.take(gathered, row_ids, axis=2)
         current = jnp.where(segment_ordinal == 0, start_state, arriving)
         onehot = (setting_ids[None, :] == pattern[:, None]).astype(jnp.float32)

time: 623 us -> 786 us (1.26)
  waiting for transfers between devices: 192 us -> 461 us
  blocking collectives: 151 us -> 18.5 us
  starting transfers between devices: 21.7 us -> 46.3 us
    ppermute x0 -> x49, waiting for transfers between devices: none -> 241 us  [end_scales_on_mesh(): lax.ppermute(now[0], axis_name=named_axis, perm=gallery)]
    all_gather x7 -> x0, blocking collectives: 133 us -> none  [advance(): gathered = lax.all_gather(incoming, 'stem', axis=2, tiled=True)]
    reduce_scatter x7, waiting for transfers between devices: 172 us -> 199 us  [advance(): lax.psum_scatter(partial_value, 'stem', scatter_dimension=2, tiled=True)]
    ppermute x0 -> x49, starting transfers between devices: none -> 24.6 us  [end_scales_on_mesh(): lax.ppermute(now[0], axis_name=named_axis, perm=gallery)]
    while x14 -> x126, local copies, waits for them, and re-layouts: 0.03 us -> 8.09 us
  transfers between devices with their start and end apart: 14 -> 63, of which waited for: 14 -> 63; matrix products, arithmetic and copies ran while one was open for 2% -> 1% of each run, Pallas kernels for 0% -> 0%
where the time goes in v1:
time: 786 us; the launch traced here: 785 us
  waiting for transfers between devices  461 us (59%)
  matrix products  178 us (23%)
  local copies, waits for them, and re-layouts  46.7 us (6%)
  starting transfers between devices  46.3 us (6%)
  other arithmetic  20.1 us (3%)
  blocking collectives  18.5 us (2%)
  between operations  13.5 us (2%)
    ppermute x49, waiting for transfers between devices, end_scales_on_mesh(): lax.ppermute(now[0], axis_name=named_axis, perm=gallery)  241 us
    reduce_scatter x7, waiting for transfers between devices, advance(): lax.psum_scatter(partial_value, 'stem', scatter_dimension=2, tiled=True)  199 us
    dot_general x7, matrix products, advance(): prod_imag = jnp.dot(expanded, weight_imag, precision=lax.Precision.HIGHEST)  97.4 us
    dot_general x7, matrix products, advance(): prod_real = jnp.dot(expanded, weight_real, precision=lax.Precision.HIGHEST)  71.4 us
    ppermute x49, starting transfers between devices, end_scales_on_mesh(): lax.ppermute(now[0], axis_name=named_axis, perm=gallery)  24.6 us
    ppermute x7, starting transfers between devices, from_behind(): return lax.ppermute(block, axis, route)  21.7 us
    another operation x1, local copies, waits for them, and re-layouts, local(): weight_imag = stem_tensor[0, 1].reshape(local_rows * settings_count, width)  21.2 us
    ppermute x7, waiting for transfers between devices, from_behind(): return lax.ppermute(block, axis, route)  20.6 us
  transfers between devices with their start and end apart: 63, of which 63 were waited for; matrix products, arithmetic and copies ran while one was open for 1% of the time, Pallas kernels for 0%

profile of v1, /device:TPU:5, one launch (start us, length us, event | category | flops | bytes accessed | tf_op | source)
XLA Modules:
  0.0 785.3 jit_solution(15490271923993913424)
XLA Ops:
  9.3 21.2 %slice_bitcast_fusion = (f32[2048,2048]{1,0:T(8,128)}, f32[2048,2048]{1,0:T(8,128)}) fusion(f32[1,2,256,8,2048]{4,3,2,1,0:T(8,128)} %param.9), kind=kLoop, calls=%fused_computation.47 | loop fusion | bytes 67108864 | tf_op jit(solution)/shard_map/reshape;squeeze | solution.py:26
  30.6 729.4 %while.18 = (s32[]{:T(128)}, f32[2,32,256]{2,1,0:T(8,128)S(1)}, f32[2,4,32]{2,1,0:T(4,128)S(1)}, pred[]{:T(512)}, s32[256]{0:T(256)S(1)}, /*index=5*/s32[]{:T(12...) while((s32[]{:T(128)}, f32[2,32,256]{2,1,0:T(8,128)S(1)}, ...), condition=%wide.region_3.4_spmd.clone, body=%wide.region_1.3_spmd.clone.sunk | while | flops 6446288896 | bytes 117491664 | solution.py:90
  70.3 13.9 %fusion.51 = f32[64,2048]{1,0:T(8,128)S(1)} fusion(f32[64,2048]{0,1:T(8,128)S(1)} %mul.87, f32[2048,2048]{1,0:T(8,128)} %get-tuple-element.499), kind=kOutput, calls=%fused_computation.59.clone.1 | convolution fusion | flops 3221225472 | bytes 17825792 | tf_op jit(solution)/shard_map/while/body/eval_jaxpr/dot_general | solution.py:69
  84.3 10.2 %fusion.52 = f32[64,2048]{1,0:T(8,128)S(1)} fusion(f32[64,2048]{0,1:T(8,128)S(1)} %mul.87, f32[2048,2048]{1,0:T(8,128)S(1)} %copy-done), kind=kOutput, calls=%fused_computation.58.clone.1 | convolution fusion | flops 3221225472 | bytes 17825792 | tf_op jit(solution)/shard_map/while/body/eval_jaxpr/dot_general | solution.py:68
  96.8 29.2 %reduce-scatter.2.cloned.1.call-done = f32[2,32,256]{2,1,0:T(8,128)} async-done(((f32[2,32,2048]{2,1,0:T(8,128)}), f32[2,32,256]{2,1,0:T(8,128)}) %reduce-scatter.2.cloned.1.call-update) | async-done | bytes 65552 | tf_op jit(solution)/shard_map/while/body/eval_jaxpr/reduce_scatter | solution.py:83
  175.9 13.9 %fusion.51 = f32[64,2048]{1,0:T(8,128)S(1)} fusion(f32[64,2048]{0,1:T(8,128)S(1)} %mul.87, f32[2048,2048]{1,0:T(8,128)} %get-tuple-element.499), kind=kOutput, calls=%fused_computation.59.clone.1 | convolution fusion | flops 3221225472 | bytes 17825792 | tf_op jit(solution)/shard_map/while/body/eval_jaxpr/dot_general | solution.py:69
  189.9 10.2 %fusion.52 = f32[64,2048]{1,0:T(8,128)S(1)} fusion(f32[64,2048]{0,1:T(8,128)S(1)} %mul.87, f32[2048,2048]{1,0:T(8,128)S(1)} %copy-done), kind=kOutput, calls=%fused_computation.58.clone.1 | convolution fusion | flops 3221225472 | bytes 17825792 | tf_op jit(solution)/shard_map/while/body/eval_jaxpr/dot_general | solution.py:68
  202.3 28.3 %reduce-scatter.2.cloned.1.call-done = f32[2,32,256]{2,1,0:T(8,128)} async-done(((f32[2,32,2048]{2,1,0:T(8,128)}), f32[2,32,256]{2,1,0:T(8,128)}) %reduce-scatter.2.cloned.1.call-update) | async-done | bytes 65552 | tf_op jit(solution)/shard_map/while/body/eval_jaxpr/reduce_scatter | solution.py:83
  280.6 13.9 %fusion.51 = f32[64,2048]{1,0:T(8,128)S(1)} fusion(f32[64,2048]{0,1:T(8,128)S(1)} %mul.87, f32[2048,2048]{1,0:T(8,128)} %get-tuple-element.499), kind=kOutput, calls=%fused_computation.59.clone.1 | convolution fusion | flops 3221225472 | bytes 17825792 | tf_op jit(solution)/shard_map/while/body/eval_jaxpr/dot_general | solution.py:69
  294.5 10.2 %fusion.52 = f32[64,2048]{1,0:T(8,128)S(1)} fusion(f32[64,2048]{0,1:T(8,128)S(1)} %mul.87, f32[2048,2048]{1,0:T(8,128)S(1)} %copy-done), kind=kOutput, calls=%fused_computation.58.clone.1 | convolution fusion | flops 3221225472 | bytes 17825792 | tf_op jit(solution)/shard_map/while/body/eval_jaxpr/dot_general | solution.py:68
  307.0 28.3 %reduce-scatter.2.cloned.1.call-done = f32[2,32,256]{2,1,0:T(8,128)} async-done(((f32[2,32,2048]{2,1,0:T(8,128)}), f32[2,32,256]{2,1,0:T(8,128)}) %reduce-scatter.2.cloned.1.call-update) | async-done | bytes 65552 | tf_op jit(solution)/shard_map/while/body/eval_jaxpr/reduce_scatter | solution.py:83
  385.3 13.9 %fusion.51 = f32[64,2048]{1,0:T(8,128)S(1)} fusion(f32[64,2048]{0,1:T(8,128)S(1)} %mul.87, f32[2048,2048]{1,0:T(8,128)} %get-tuple-element.499), kind=kOutput, calls=%fused_computation.59.clone.1 | convolution fusion | flops 3221225472 | bytes 17825792 | tf_op jit(solution)/shard_map/while/body/eval_jaxpr/dot_general | solution.py:69
  399.2 10.2 %fusion.52 = f32[64,2048]{1,0:T(8,128)S(1)} fusion(f32[64,2048]{0,1:T(8,128)S(1)} %mul.87, f32[2048,2048]{1,0:T(8,128)S(1)} %copy-done), kind=kOutput, calls=%fused_computation.58.clone.1 | convolution fusion | flops 3221225472 | bytes 17825792 | tf_op jit(solution)/shard_map/while/body/eval_jaxpr/dot_general | solution.py:68
  411.7 28.2 %reduce-scatter.2.cloned.1.call-done = f32[2,32,256]{2,1,0:T(8,128)} async-done(((f32[2,32,2048]{2,1,0:T(8,128)}), f32[2,32,256]{2,1,0:T(8,128)}) %reduce-scatter.2.cloned.1.call-update) | async-done | bytes 65552 | tf_op jit(solution)/shard_map/while/body/eval_jaxpr/reduce_scatter | solution.py:83
  489.8 13.9 %fusion.51 = f32[64,2048]{1,0:T(8,128)S(1)} fusion(f32[64,2048]{0,1:T(8,128)S(1)} %mul.87, f32[2048,2048]{1,0:T(8,128)} %get-tuple-element.499), kind=kOutput, calls=%fused_computation.59.clone.1 | convolution fusion | flops 3221225472 | bytes 17825792 | tf_op jit(solution)/shard_map/while/body/eval_jaxpr/dot_general | solution.py:69
  503.8 10.2 %fusion.52 = f32[64,2048]{1,0:T(8,128)S(1)} fusion(f32[64,2048]{0,1:T(8,128)S(1)} %mul.87, f32[2048,2048]{1,0:T(8,128)S(1)} %copy-done), kind=kOutput, calls=%fused_computation.58.clone.1 | convolution fusion | flops 3221225472 | bytes 17825792 | tf_op jit(solution)/shard_map/while/body/eval_jaxpr/dot_general | solution.py:68
  516.3 28.3 %reduce-scatter.2.cloned.1.call-done = f32[2,32,256]{2,1,0:T(8,128)} async-done(((f32[2,32,2048]{2,1,0:T(8,128)}), f32[2,32,256]{2,1,0:T(8,128)}) %reduce-scatter.2.cloned.1.call-update) | async-done | bytes 65552 | tf_op jit(solution)/shard_map/while/body/eval_jaxpr/reduce_scatter | solution.py:83
  594.6 13.9 %fusion.51 = f32[64,2048]{1,0:T(8,128)S(1)} fusion(f32[64,2048]{0,1:T(8,128)S(1)} %mul.87, f32[2048,2048]{1,0:T(8,128)} %get-tuple-element.499), kind=kOutput, calls=%fused_computation.59.clone.1 | convolution fusion | flops 3221225472 | bytes 17825792 | tf_op jit(solution)/shard_map/while/body/eval_jaxpr/dot_general | solution.py:69
  608.5 10.2 %fusion.52 = f32[64,2048]{1,0:T(8,128)S(1)} fusion(f32[64,2048]{0,1:T(8,128)S(1)} %mul.87, f32[2048,2048]{1,0:T(8,128)S(1)} %copy-done), kind=kOutput, calls=%fused_computation.58.clone.1 | convolution fusion | flops 3221225472 | bytes 17825792 | tf_op jit(solution)/shard_map/while/body/eval_jaxpr/dot_general | solution.py:68
  621.0 28.3 %reduce-scatter.2.cloned.1.call-done = f32[2,32,256]{2,1,0:T(8,128)} async-done(((f32[2,32,2048]{2,1,0:T(8,128)}), f32[2,32,256]{2,1,0:T(8,128)}) %reduce-scatter.2.cloned.1.call-update) | async-done | bytes 65552 | tf_op jit(solution)/shard_map/while/body/eval_jaxpr/reduce_scatter | solution.py:83
  699.2 13.9 %fusion.51 = f32[64,2048]{1,0:T(8,128)S(1)} fusion(f32[64,2048]{0,1:T(8,128)S(1)} %mul.87, f32[2048,2048]{1,0:T(8,128)} %get-tuple-element.499), kind=kOutput, calls=%fused_computation.59.clone.1 | convolution fusion | flops 3221225472 | bytes 17825792 | tf_op jit(solution)/shard_map/while/body/eval_jaxpr/dot_general | solution.py:69
  713.2 10.2 %fusion.52 = f32[64,2048]{1,0:T(8,128)S(1)} fusion(f32[64,2048]{0,1:T(8,128)S(1)} %mul.87, f32[2048,2048]{1,0:T(8,128)S(1)} %copy-done), kind=kOutput, calls=%fused_computation.58.clone.1 | convolution fusion | flops 3221225472 | bytes 17825792 | tf_op jit(solution)/shard_map/while/body/eval_jaxpr/dot_general | solution.py:68
  725.7 28.3 %reduce-scatter.2.cloned.1.call-done = f32[2,32,256]{2,1,0:T(8,128)} async-done(((f32[2,32,2048]{2,1,0:T(8,128)}), f32[2,32,256]{2,1,0:T(8,128)}) %reduce-scatter.2.cloned.1.call-update) | async-done | bytes 65552 | tf_op jit(solution)/shard_map/while/body/eval_jaxpr/reduce_scatter | solution.py:83
  760.0 18.5 %psum.7 = f32[1,2,4,32]{3,2,1,0:T(4,128)} all-reduce(f32[1,2,4,32]{3,2,1,0:T(4,128)S(1)} %bitcast.124), channel_id=1, replica_groups=mesh['section'=4,'stem'=8] {'stem'}, use_global_device_ids=true, to_apply=%region_4.5 | all-reduce | flops 256 | bytes 2048 | tf_op jit(solution)/shard_map/psum | solution.py:91
  (407 shorter events, 362.8 us)
Async XLA Ops:
  30.6 95.3 %reduce-scatter.2.cloned.1.call-start = ((), (), s32[]{:S(2)}) async-start(), calls=%async_computation.1 | async-start | bytes 589824 | tf_op jit(solution)/shard_map/while/body/eval_jaxpr/reduce_scatter | solution.py:83
  125.9 6.1 collective-permute-start.7
  132.1 98.6 %reduce-scatter.2.cloned.1.call-start = ((), (), s32[]{:S(2)}) async-start(), calls=%async_computation.1 | async-start | bytes 589824 | tf_op jit(solution)/shard_map/while/body/eval_jaxpr/reduce_scatter | solution.py:83
  132.1 5.7 collective-permute-start
  137.7 5.5 collective-permute-start.1
  230.6 6.1 collective-permute-start.7
  236.7 98.6 %reduce-scatter.2.cloned.1.call-start = ((), (), s32[]{:S(2)}) async-start(), calls=%async_computation.1 | async-start | bytes 589824 | tf_op jit(solution)/shard_map/while/body/eval_jaxpr/reduce_scatter | solution.py:83
  236.7 5.7 collective-permute-start
  242.4 5.5 collective-permute-start.1
  335.3 6.1 collective-permute-start.7
  341.4 98.4 %reduce-scatter.2.cloned.1.call-start = ((), (), s32[]{:S(2)}) async-start(), calls=%async_computation.1 | async-start | bytes 589824 | tf_op jit(solution)/shard_map/while/body/eval_jaxpr/reduce_scatter | solution.py:83
  341.4 5.7 collective-permute-start
  347.1 5.5 collective-permute-start.1
  439.8 6.1 collective-permute-start.7
  445.9 98.7 %reduce-scatter.2.cloned.1.call-start = ((), (), s32[]{:S(2)}) async-start(), calls=%async_computation.1 | async-start | bytes 589824 | tf_op jit(solution)/shard_map/while/body/eval_jaxpr/reduce_scatter | solution.py:83
  445.9 5.7 collective-permute-start
  451.6 5.5 collective-permute-start.1
  544.6 6.1 collective-permute-start.7
  550.7 98.5 %reduce-scatter.2.cloned.1.call-start = ((), (), s32[]{:S(2)}) async-start(), calls=%async_computation.1 | async-start | bytes 589824 | tf_op jit(solution)/shard_map/while/body/eval_jaxpr/reduce_scatter | solution.py:83
  550.7 5.7 collective-permute-start
  649.3 6.1 collective-permute-start.7
  655.4 98.5 %reduce-scatter.2.cloned.1.call-start = ((), (), s32[]{:S(2)}) async-start(), calls=%async_computation.1 | async-start | bytes 589824 | tf_op jit(solution)/shard_map/while/body/eval_jaxpr/reduce_scatter | solution.py:83
  655.4 5.7 collective-permute-start
  753.9 6.1 collective-permute-start.7
  (48 other events, 350.0 us)
Sparse Core Ops, SparseCore 0:
  95.5 30.3 reduce-scatter.1
  201.1 29.4 reduce-scatter.1
  305.8 29.4 reduce-scatter.1
  410.5 29.3 reduce-scatter.1
  515.0 29.5 reduce-scatter.1
  619.8 29.4 reduce-scatter.1
  724.4 29.4 reduce-scatter.1
